TPU v7x, 32 devices: a whole 2x2x4 slice. The times are simulated.
32 devices in a mesh: seq: 8 (over y, x, core), head: 4 (over z).
Axes of the slice: x: 2, y: 2, z: 4, core: 2. Of those that a mesh axis runs over, the one named last changes fastest.
Arguments:
- latent: bfloat16 [8, 1024, 2048], P('seq', None, 'head'), may hold values from -6 to 6
- modulation: float32 [9, 2048], replicated, may hold values from -3 to 3
- spatial_qkv: bfloat16 [3, 2048, 2048], P(None, None, 'head')
- spatial_out: bfloat16 [2048, 2048], P('head'), may hold values from -0.125 to 0.125
- temporal_qkv: bfloat16 [3, 2048, 2048], P(None, None, 'head')
- temporal_out: bfloat16 [2048, 2048], P('head'), may hold values from -0.125 to 0.125
- hidden_weight: bfloat16 [2048, 8192], P(None, 'head'), may hold values from -0.125 to 0.125
- output_weight: bfloat16 [8192, 2048], P('head'), may hold values from -0.0625 to 0.0625
Outputs:
- block_out: bfloat16 [8, 1024, 2048], P(None, 'seq', 'head')
All inputs are finite; a program needn't handle non-finite values.
Results may differ from a plain program's by a relative error of at most 0.009.
Values may be sent and summed in bfloat16 or wider, within the bound.
A program may use at most 128 MiB of HBM per device.

v0:
```python
import functools
import math

import jax
import jax.numpy as jnp
from jax import lax
from jax.experimental import pallas as pl
from jax.experimental.pallas import tpu as pltpu
from jax.sharding import PartitionSpec as P

HD = 64
PAIR = 128
CHUNKS = 2
EXP2_SCALE = HD ** (-0.5) * math.log2(math.e)
BF16 = jnp.bfloat16
NT = (((1,), (1,)), ((), ()))


def layer_norm(values):
    average = jnp.mean(values, axis=-1, keepdims=True)
    centred = values - average
    variance = jnp.mean(centred * centred, axis=-1, keepdims=True)
    return centred * lax.rsqrt(variance + 1e-06)


def modulate(stream, modulation, offset):
    normed = layer_norm(stream.astype(jnp.float32))
    return (normed * (1.0 + modulation[offset + 1]) + modulation[offset]).astype(BF16)


def weighted_values(scores, values):
    top = jnp.max(scores, axis=-1, keepdims=True)
    weights = jnp.exp2((scores - top) * EXP2_SCALE).astype(BF16)
    extended = jnp.concatenate([values, jnp.ones_like(values)], axis=1)
    summed = jnp.dot(weights, extended, preferred_element_type=jnp.float32)
    return summed[:, :HD] / summed[:, HD:]


def spatial_kernel(q_ref, k_ref, v_ref, o_ref):
    outs = []
    for head in range(PAIR // HD):
        lanes = slice(head * HD, (head + 1) * HD)
        scores = lax.dot_general(
            q_ref[0, :, lanes], k_ref[0, :, lanes], NT, preferred_element_type=jnp.float32
        )
        outs.append(weighted_values(scores, v_ref[0, :, lanes]))
    o_ref[0] = jnp.concatenate(outs, axis=1).astype(BF16)


def spatial_attention(query, keys, values):
    frames, patches, width = query.shape
    rows = min(patches, 512)
    total = keys.shape[1]
    return pl.pallas_call(
        spatial_kernel,
        grid=(frames, width // PAIR, patches // rows),
        in_specs=[
            pl.BlockSpec((1, rows, PAIR), lambda f, h, r: (f, r, h)),
            pl.BlockSpec((1, total, PAIR), lambda f, h, r: (f, 0, h)),
            pl.BlockSpec((1, total, PAIR), lambda f, h, r: (f, 0, h)),
        ],
        out_specs=pl.BlockSpec((1, rows, PAIR), lambda f, h, r: (f, r, h)),
        out_shape=jax.ShapeDtypeStruct(query.shape, BF16),
        cost_estimate=pl.CostEstimate(
            flops=16 * frames * patches * total * width,
            bytes_accessed=8 * query.size,
            transcendentals=frames * patches * total * (width // HD),
        ),
        name="spatial_attention",
    )(query, keys, values)


def temporal_kernel(q_ref, k_ref, v_ref, o_ref):
    frames, group, width = q_ref.shape
    rows = frames * group
    query = q_ref[...].reshape(rows, width)
    keys = k_ref[...].reshape(rows, width)
    values = v_ref[...].reshape(rows, width)
    first = lax.broadcasted_iota(jnp.int32, (rows, rows), 0)
    second = lax.broadcasted_iota(jnp.int32, (rows, rows), 1)
    same_patch = lax.rem(first, group) == lax.rem(second, group)
    outs = []
    for head in range(width // HD):
        lanes = slice(head * HD, (head + 1) * HD)
        scores = lax.dot_general(
            query[:, lanes], keys[:, lanes], NT, preferred_element_type=jnp.float32
        )
        outs.append(
            weighted_values(jnp.where(same_patch, scores, -jnp.inf), values[:, lanes])
        )
    o_ref[...] = jnp.concatenate(outs, axis=1).astype(BF16).reshape(frames, group, width)


def temporal_attention(query, keys, values):
    frames, patches, width = query.shape
    group = min(16, patches)
    spec = pl.BlockSpec((frames, group, width), lambda g: (0, g, 0))
    return pl.pallas_call(
        temporal_kernel,
        grid=(patches // group,),
        in_specs=[spec] * 3,
        out_specs=spec,
        out_shape=jax.ShapeDtypeStruct(query.shape, BF16),
        cost_estimate=pl.CostEstimate(
            flops=16 * frames * frames * patches * group * width,
            bytes_accessed=8 * query.size,
            transcendentals=frames * frames * patches * group * (width // HD),
        ),
        name="temporal_attention",
    )(query, keys, values)


def project_three(normed, weights):
    return [
        jnp.dot(normed, weights[member], preferred_element_type=jnp.float32).astype(BF16)
        for member in range(3)
    ]


def summed_columns(portion, row_block):
    partial = jnp.dot(portion, row_block, preferred_element_type=jnp.float32).astype(BF16)
    return lax.psum_scatter(partial, "head", scatter_dimension=2, tiled=True)


def add_branch(stream, gate, reduced):
    return (stream.astype(jnp.float32) + gate * reduced.astype(jnp.float32)).astype(BF16)


def per_device(
    latent,
    modulation,
    spatial_qkv,
    spatial_out,
    temporal_qkv,
    temporal_out,
    hidden_weight,
    output_weight,
):
    frames_local, patches, width_local = latent.shape
    seq = lax.axis_size("seq")
    patches_local = patches // seq
    piece = patches_local // CHUNKS
    anchor = lax.axis_index("head") * width_local
    local_rows = lax.dynamic_slice_in_dim(modulation, anchor, width_local, 1)
    full_spatial = lax.all_gather(latent, "head", axis=2, tiled=True)
    normed = modulate(full_spatial, modulation, 0)
    query, keys, values = project_three(normed, spatial_qkv)

    def chunk_of(tensor, index):
        parts = tensor.reshape(frames_local, seq, CHUNKS, piece, width_local)
        return parts[:, :, index].reshape(frames_local, seq * piece, width_local)

    outs = []
    ones = []
    for index in range(CHUNKS):
        spatial = spatial_attention(chunk_of(query, index), keys, values)
        reduced = summed_columns(spatial, spatial_out)
        if ones:
            ones[-1], reduced = lax.optimization_barrier((ones[-1], reduced))
        one = add_branch(chunk_of(latent, index), local_rows[2], reduced)
        ones.append(lax.all_to_all(one, "seq", split_axis=1, concat_axis=0, tiled=True))
    twos = []
    for one in ones:
        full = lax.all_gather(one, "head", axis=2, tiled=True)
        normed = modulate(full, modulation, 3)
        temporal = temporal_attention(*project_three(normed, temporal_qkv))
        reduced = summed_columns(temporal, temporal_out)
        twos.append(add_branch(one, local_rows[5], reduced))
    for two in twos:
        full = lax.all_gather(two, "head", axis=2, tiled=True)
        normed = modulate(full, modulation, 6)
        pre_act = jnp.dot(normed, hidden_weight, preferred_element_type=jnp.float32)
        hidden = jax.nn.gelu(pre_act, approximate=True).astype(BF16)
        reduced = summed_columns(hidden, output_weight)
        outs.append(add_branch(two, local_rows[8], reduced))
    return jnp.concatenate(outs, axis=1)


def solution(mesh):
    in_specs = (
        P("seq", None, "head"),
        P(),
        P(None, None, "head"),
        P("head", None),
        P(None, None, "head"),
        P("head", None),
        P(None, "head"),
        P("head", None),
    )
    out_specs = P(None, "seq", "head")
    return jax.shard_map(
        per_device, mesh=mesh, in_specs=in_specs, out_specs=out_specs, check_vma=False
    )
```

profile of v0, /device:TPU:0, one launch (start us, length us, event | category | flops | bytes accessed | tf_op | source)
XLA Modules:
  0.0 585.5 jit_solution(13023405403565005239)
XLA Ops:
  8.4 84.0 %all-gather.6.cloned.1.call-done = bf16[1,1024,2048]{2,1,0:T(8,128)(2,1)} async-done(((bf16[1,1024,512]{2,1,0:T(8,128)(2,1)}), bf16[1,1024,2048]{2,1,0:T(8,128)(2,1)}) %all-gather.6.cloned.1.call-update) | async-done | bytes 4194320 | tf_op jit(solution)/shard_map/all_gather | solution.py:145
  92.4 3.0 convert_reduce_fusion
  97.1 1.9 fusion.54
  99.4 2.3 fusion.106
  101.7 3.3 fusion.115.v_ref
  105.0 3.3 fusion.118.k_ref
  109.4 10.2 %spatial_attention.2 = bf16[1,512,512]{2,1,0:T(8,128)(2,1)} custom-call(bf16[1,512,512]{2,1,0:T(8,128)(2,1)} %bitcast.145, bf16[1,1024,512]{2,1,0:T(8,128)(2,1)} %fusion.118.k_ref, bf16[1,1024,512]{2,1,0:T(8,128)(2,1)} %fusion.115.v_ref), custom_call_target="tpu_custom_call" | custom-call | flops 4294967296 | bytes 2097152 | tf_op jit(solution)/shard_map/spatial_attention/pallas_call | solution.py:54
  119.6 3.6 fusion.65
  123.6 10.2 %spatial_attention.3 = bf16[1,512,512]{2,1,0:T(8,128)(2,1)} custom-call(bf16[1,512,512]{2,1,0:T(8,128)(2,1)} %bitcast.144, bf16[1,1024,512]{2,1,0:T(8,128)(2,1)} %fusion.118.k_ref, bf16[1,1024,512]{2,1,0:T(8,128)(2,1)} %fusion.115.v_ref), custom_call_target="tpu_custom_call" | custom-call | flops 4294967296 | bytes 2097152 | tf_op jit(solution)/shard_map/spatial_attention/pallas_call | solution.py:54
  133.8 3.7 fusion.66
  139.3 26.1 %reduce-scatter.7.cloned.1.call-done = bf16[1,512,512]{2,1,0:T(8,128)(2,1)} async-done(((bf16[1,512,2048]{2,1,0:T(8,128)(2,1)}), bf16[1,512,512]{2,1,0:T(8,128)(2,1)}) %reduce-scatter.7.cloned.1.call-update) | async-done | bytes 524304 | tf_op jit(solution)/shard_map/reduce_scatter | solution.py:122
  168.1 3.8 reduce.2
  172.3 13.2 %all_to_all.24 = bf16[8,2,16384]{2,1,0:T(2,128)(2,1)S(1)} all-to-all(bf16[8,2,16384]{2,1,0:T(2,128)(2,1)S(1)} %reshape.180), channel_id=1, replica_groups=mesh['seq'=8,'head'=4] {'seq'}, dimensions={0} | all-to-all | bytes 1048576 | tf_op jit(solution)/shard_map/all_to_all | solution.py:161
  186.9 23.7 %reduce-scatter.9.cloned.1.call-done = bf16[1,512,512]{2,1,0:T(8,128)(2,1)} async-done(((bf16[1,512,2048]{2,1,0:T(8,128)(2,1)}), bf16[1,512,512]{2,1,0:T(8,128)(2,1)}) %reduce-scatter.9.cloned.1.call-update) | async-done | bytes 524304 | tf_op jit(solution)/shard_map/reduce_scatter | solution.py:122
  213.3 3.8 reduce.3
  217.4 13.2 %all_to_all.25 = bf16[8,2,16384]{2,1,0:T(2,128)(2,1)S(1)} all-to-all(bf16[8,2,16384]{2,1,0:T(2,128)(2,1)S(1)} %reshape.182), channel_id=1, replica_groups=mesh['seq'=8,'head'=4] {'seq'}, dimensions={0} | all-to-all | bytes 1048576 | tf_op jit(solution)/shard_map/all_to_all | solution.py:161
  232.3 24.6 %all-gather.8.cloned.1.call-done = bf16[8,64,2048]{2,1,0:T(8,128)(2,1)} async-done(((bf16[8,64,512]{2,1,0:T(8,128)(2,1)}), bf16[8,64,2048]{2,1,0:T(8,128)(2,1)}) %all-gather.8.cloned.1.call-update) | async-done | bytes 2097168 | tf_op jit(solution)/shard_map/all_gather | solution.py:164
  257.0 2.1 convert_reduce_fusion.4
  259.1 2.4 fusion.34
  261.5 3.9 fusion.133.v_ref
  265.4 2.1 fusion.127.k_ref
  267.5 2.1 fusion.121.q_ref
  269.6 10.8 %temporal_attention.2 = bf16[8,64,512]{2,1,0:T(8,128)(2,1)} custom-call(bf16[8,64,512]{2,1,0:T(8,128)(2,1)} %fusion.121.q_ref, bf16[8,64,512]{2,1,0:T(8,128)(2,1)} %fusion.127.k_ref, bf16[8,64,512]{2,1,0:T(8,128)(2,1)} %fusion.133.v_ref), custom_call_target="tpu_custom_call" | custom-call | flops 536870912 | bytes 2097152 | tf_op jit(solution)/shard_map/temporal_attention/pallas_call | solution.py:98
  280.4 4.4 convolution_convert_fusion.1
  285.1 17.8 %all-gather.12.cloned.1.call-done = bf16[8,64,2048]{2,1,0:T(8,128)(2,1)} async-done(((bf16[8,64,512]{2,1,0:T(8,128)(2,1)}), bf16[8,64,2048]{2,1,0:T(8,128)(2,1)}) %all-gather.12.cloned.1.call-update) | async-done | bytes 2097168 | tf_op jit(solution)/shard_map/all_gather | solution.py:164
  302.9 2.1 convert_reduce_fusion.2
  305.0 2.4 fusion.26
  307.4 3.9 fusion.136.v_ref
  311.3 2.1 fusion.130.k_ref
  313.4 2.1 fusion.124.q_ref
  315.5 10.8 %temporal_attention.3 = bf16[8,64,512]{2,1,0:T(8,128)(2,1)} custom-call(bf16[8,64,512]{2,1,0:T(8,128)(2,1)} %fusion.124.q_ref, bf16[8,64,512]{2,1,0:T(8,128)(2,1)} %fusion.130.k_ref, bf16[8,64,512]{2,1,0:T(8,128)(2,1)} %fusion.136.v_ref), custom_call_target="tpu_custom_call" | custom-call | flops 536870912 | bytes 2097152 | tf_op jit(solution)/shard_map/temporal_attention/pallas_call | solution.py:98
  326.3 4.4 convolution_convert_fusion
  330.8 16.7 %reduce-scatter.11.cloned.1.call-done = bf16[8,64,512]{2,1,0:T(8,128)(2,1)} async-done(((bf16[8,64,2048]{2,1,0:T(8,128)(2,1)}), bf16[8,64,512]{2,1,0:T(8,128)(2,1)}) %reduce-scatter.11.cloned.1.call-update) | async-done | bytes 524304 | tf_op jit(solution)/shard_map/reduce_scatter | solution.py:122
  347.5 45.1 %reduce-scatter.15.cloned.1.call-done = bf16[8,64,512]{2,1,0:T(8,128)(2,1)} async-done(((bf16[8,64,2048]{2,1,0:T(8,128)(2,1)}), bf16[8,64,512]{2,1,0:T(8,128)(2,1)}) %reduce-scatter.15.cloned.1.call-update) | async-done | bytes 524304 | tf_op jit(solution)/shard_map/reduce_scatter | solution.py:122
  392.6 2.5 add_convert_fusion.3
  396.2 44.0 %all-gather.14.cloned.1.call-done = bf16[8,64,2048]{2,1,0:T(8,128)(2,1)} async-done(((bf16[8,64,512]{2,1,0:T(8,128)(2,1)}), bf16[8,64,2048]{2,1,0:T(8,128)(2,1)}) %all-gather.14.cloned.1.call-update) | async-done | bytes 2097168 | tf_op jit(solution)/shard_map/all_gather | solution.py:170
  440.2 2.1 convert_reduce_fusion.1
  442.3 2.6 fusion.22
  444.9 9.5 %fusion.53 = bf16[8,64,2048]{2,1,0:T(8,128)(2,1)S(1)} fusion(bf16[2048,2048]{1,0:T(8,128)(2,1)} %param.14, bf16[8,64,2048]{2,1,0:T(8,128)(2,1)S(1)} %copy-done.6, f32[8,64]{1,0:T(8,128)S(1)} %add_rsqrt_fusion, f32[8,64]{1,0:T(8,128)S(1)} %broadcast_multiply_fusion, f32[2048]{0:T(1024)S(1)} %bitcast.152, f32[2048]{0:T(1024)S(1)} %bitcast.150), kind=kOutput, calls=%fused_computation.65 | convolution fusion | flops 4310695936 | bytes 12603392 | tf_op jit(solution)/shard_map/dot_general | solution.py:172
  454.5 5.7 fusion.58
  460.3 26.0 %all-gather.10.cloned.1.call-done = bf16[8,64,2048]{2,1,0:T(8,128)(2,1)} async-done(((bf16[8,64,512]{2,1,0:T(8,128)(2,1)}), bf16[8,64,2048]{2,1,0:T(8,128)(2,1)}) %all-gather.10.cloned.1.call-update) | async-done | bytes 2097168 | tf_op jit(solution)/shard_map/all_gather | solution.py:170
  486.2 2.1 convert_reduce_fusion.3
  488.3 2.6 fusion.30
  491.0 9.6 %fusion.45 = bf16[8,64,2048]{2,1,0:T(8,128)(2,1)S(1)} fusion(bf16[2048,2048]{1,0:T(8,128)(2,1)} %param.14, bf16[8,64,2048]{2,1,0:T(8,128)(2,1)S(1)} %copy-done.5, f32[2048]{0:T(1024)S(1)} %bitcast.153, f32[2048]{0:T(1024)S(1)} %bitcast.151, f32[8,64]{1,0:T(8,128)S(1)} %add_rsqrt_fusion.2, f32[8,64]{1,0:T(8,128)S(1)} %broadcast_multiply_fusion.2), kind=kOutput, calls=%fused_computation.57 | convolution fusion | flops 4310695936 | bytes 12603392 | tf_op jit(solution)/shard_map/dot_general | solution.py:172
  500.7 5.7 fusion.55
  506.4 24.4 %reduce-scatter.17.cloned.1.call-done = bf16[8,64,512]{2,1,0:T(8,128)(2,1)} async-done(((bf16[8,64,2048]{2,1,0:T(8,128)(2,1)}), bf16[8,64,512]{2,1,0:T(8,128)(2,1)}) %reduce-scatter.17.cloned.1.call-update) | async-done | bytes 524304 | tf_op jit(solution)/shard_map/reduce_scatter | solution.py:122
  530.8 45.2 %reduce-scatter.13.cloned.1.call-done = bf16[8,64,512]{2,1,0:T(8,128)(2,1)} async-done(((bf16[8,64,2048]{2,1,0:T(8,128)(2,1)}), bf16[8,64,512]{2,1,0:T(8,128)(2,1)}) %reduce-scatter.13.cloned.1.call-update) | async-done | bytes 524304 | tf_op jit(solution)/shard_map/reduce_scatter | solution.py:122
  576.0 1.5 add_convert_fusion.2
  (100 shorter events, 18.9 us)
Async XLA Ops:
  6.5 113.0 %copy-start = (bf16[512,2048]{1,0:T(8,128)(2,1)S(1)}, bf16[512,2048]{1,0:T(8,128)(2,1)}, u32[]{:S(2)}) copy-start(bf16[512,2048]{1,0:T(8,128)(2,1)} %param.11) | copy-start | bytes 6291460
  6.5 85.9 %all-gather.6.cloned.1.call-start = ((), (), s32[]{:S(2)}) async-start(), calls=%async_computation.8 | async-start | bytes 5242880 | tf_op jit(solution)/shard_map/all_gather | solution.py:145
  7.3 158.2 %reduce-scatter.7.cloned.1.call-start = ((), (), s32[]{:S(2)}) async-start(), calls=%async_computation.9 | async-start | bytes 2621440 | tf_op jit(solution)/shard_map/reduce_scatter | solution.py:122
  92.4 3.4 copy-start.2
  95.8 3.1 slice-start.4
  97.1 2.3 slice-start.5
  123.2 87.4 %reduce-scatter.9.cloned.1.call-start = ((), (), s32[]{:S(2)}) async-start(), calls=%async_computation.10 | async-start | bytes 2621440 | tf_op jit(solution)/shard_map/reduce_scatter | solution.py:122
  133.8 4.7 copy-start.11
  137.5 119.4 %all-gather.8.cloned.1.call-start = ((), (), s32[]{:S(2)}) async-start(), calls=%async_computation.11 | async-start | bytes 2621440 | tf_op jit(solution)/shard_map/all_gather | solution.py:164
  166.7 44.5 %copy-start.12 = (bf16[1,8,1,64,512]{4,3,2,1,0:T(8,128)(2,1)S(1)}, bf16[1,8,1,64,512]{4,3,2,1,0:T(8,128)(2,1)}, u32[]{:S(2)}) copy-start(bf16[1,8,1,64,512]{4,3,2,1,0:T(8,128)(2,1)} %get-tuple-element.9) | copy-start | bytes 1572868
  210.7 92.2 %all-gather.12.cloned.1.call-start = ((), (), s32[]{:S(2)}) async-start(), calls=%async_computation.15 | async-start | bytes 2621440 | tf_op jit(solution)/shard_map/all_gather | solution.py:164
  232.1 115.4 %reduce-scatter.11.cloned.1.call-start = ((), (), s32[]{:S(2)}) async-start(), calls=%async_computation.12 | async-start | bytes 2621440 | tf_op jit(solution)/shard_map/reduce_scatter | solution.py:122
  257.0 4.5 copy-start.4
  259.1 6.3 %slice-start.6 = ((s8[6291456]{0:T(1024)(128)(4,1)}), s8[4194304]{0:T(1024)(128)(4,1)S(1)}, s32[]{:S(2)}) async-start(s8[6291456]{0:T(1024)(128)(4,1)} %bitcast.174), calls=%async_computation.25 | async-start | bytes 8388608
  261.5 3.9 slice-start.7
  284.8 107.8 %reduce-scatter.15.cloned.1.call-start = ((), (), s32[]{:S(2)}) async-start(), calls=%async_computation.16 | async-start | bytes 2621440 | tf_op jit(solution)/shard_map/reduce_scatter | solution.py:122
  302.9 4.5 copy-start.3
  305.0 6.3 %slice-start.8 = ((s8[6291456]{0:T(1024)(128)(4,1)}), s8[4194304]{0:T(1024)(128)(4,1)S(1)}, s32[]{:S(2)}) async-start(s8[6291456]{0:T(1024)(128)(4,1)} %bitcast.176), calls=%async_computation.27 | async-start | bytes 8388608
  307.4 3.9 slice-start.9
  326.3 66.3 %copy-start.7 = (bf16[1,512,512]{2,1,0:T(8,128)(2,1)S(1)}, bf16[1,512,512]{2,1,0:T(8,128)(2,1)}, u32[]{:S(2)}) copy-start(bf16[1,512,512]{2,1,0:T(8,128)(2,1)} %copy.25) | copy-start | bytes 1572868
  326.3 66.3 %copy-start.8 = (bf16[1,512,512]{2,1,0:T(8,128)(2,1)S(1)}, bf16[1,512,512]{2,1,0:T(8,128)(2,1)}, u32[]{:S(2)}) copy-start(bf16[1,512,512]{2,1,0:T(8,128)(2,1)} %copy.26) | copy-start | bytes 1572868
  330.8 109.4 %all-gather.14.cloned.1.call-start = ((), (), s32[]{:S(2)}) async-start(), calls=%async_computation.17 | async-start | bytes 2621440 | tf_op jit(solution)/shard_map/all_gather | solution.py:170
  395.2 91.1 %all-gather.10.cloned.1.call-start = ((), (), s32[]{:S(2)}) async-start(), calls=%async_computation.13 | async-start | bytes 2621440 | tf_op jit(solution)/shard_map/all_gather | solution.py:170
  395.9 134.9 %reduce-scatter.17.cloned.1.call-start = ((), (), s32[]{:S(2)}) async-start(), calls=%async_computation.18 | async-start | bytes 2621440 | tf_op jit(solution)/shard_map/reduce_scatter | solution.py:122
  440.2 4.8 copy-start.6
  440.2 14.3 %slice-start = ((s8[8388608]{0:T(1024)(128)(4,1)}), s8[4194304]{0:T(1024)(128)(4,1)S(1)}, s32[]{:S(2)}) async-start(s8[8388608]{0:T(1024)(128)(4,1)} %bitcast.168), calls=%async_computation.19 | async-start | bytes 8388608
  444.9 9.6 %slice-start.1 = ((s8[8388608]{0:T(1024)(128)(4,1)}), s8[4194304]{0:T(1024)(128)(4,1)S(1)}, s32[]{:S(2)}) async-start(s8[8388608]{0:T(1024)(128)(4,1)} %bitcast.168), calls=%async_computation.20 | async-start | bytes 8388608
  460.2 115.8 %reduce-scatter.13.cloned.1.call-start = ((), (), s32[]{:S(2)}) async-start(), calls=%async_computation.14 | async-start | bytes 2621440 | tf_op jit(solution)/shard_map/reduce_scatter | solution.py:122
  486.2 4.7 copy-start.5
  486.2 14.4 %slice-start.2 = ((s8[8388608]{0:T(1024)(128)(4,1)}), s8[4194304]{0:T(1024)(128)(4,1)S(1)}, s32[]{:S(2)}) async-start(s8[8388608]{0:T(1024)(128)(4,1)} %bitcast.170), calls=%async_computation.21 | async-start | bytes 8388608
  491.0 9.7 %slice-start.3 = ((s8[8388608]{0:T(1024)(128)(4,1)}), s8[4194304]{0:T(1024)(128)(4,1)S(1)}, s32[]{:S(2)}) async-start(s8[8388608]{0:T(1024)(128)(4,1)} %bitcast.170), calls=%async_computation.22 | async-start | bytes 8388608
  500.7 75.3 %copy-start.9 = (bf16[8,64,512]{2,1,0:T(8,128)(2,1)S(1)}, bf16[8,64,512]{2,1,0:T(8,128)(2,1)}, u32[]{:S(2)}) copy-start(bf16[8,64,512]{2,1,0:T(8,128)(2,1)} %get-tuple-element.24) | copy-start | bytes 1572868
  500.7 75.3 %copy-start.10 = (bf16[8,64,512]{2,1,0:T(8,128)(2,1)S(1)}, bf16[8,64,512]{2,1,0:T(8,128)(2,1)}, u32[]{:S(2)}) copy-start(bf16[8,64,512]{2,1,0:T(8,128)(2,1)} %get-tuple-element.25) | copy-start | bytes 1572868
  500.7 77.9 %copy-start.1 = (bf16[512,2048]{1,0:T(8,128)(2,1)S(1)}, bf16[512,2048]{1,0:T(8,128)(2,1)}, u32[]{:S(2)}) copy-start(bf16[512,2048]{1,0:T(8,128)(2,1)} %param.11) | copy-start | bytes 6291460
Sparse Core Ops, SparseCore 0:
  8.9 83.4 all-gather.5
  123.3 42.0 reduce-scatter.6
  167.8 42.8 reduce-scatter.8
  212.1 44.8 all-gather.7
  258.4 44.4 all-gather.11
  305.0 42.4 reduce-scatter.10
  349.8 42.8 reduce-scatter.14
  395.3 44.8 all-gather.13
  441.7 44.4 all-gather.9
  488.4 42.4 reduce-scatter.16
  533.1 42.8 reduce-scatter.12
where the time goes:
time: 594 us; the launch traced here: 586 us
  waiting for transfers between devices  379 us (64%)
  matrix products  71.8 us (12%)
  Pallas kernels  42 us (7%)
  other arithmetic  40.8 us (7%)
  blocking collectives  26.3 us (4%)
  between operations  14 us (2%)
  local copies, waits for them, and re-layouts  9.67 us (2%)
    reduce_scatter x6, waiting for transfers between devices, summed_columns(): return lax.psum_scatter(partial, 'head', scatter_dimension=2, tiled=True)  181 us
    all_gather x1, waiting for transfers between devices, per_device(): full_spatial = lax.all_gather(latent, 'head', axis=2, tiled=True)  84 us
    all_gather x2, waiting for transfers between devices, per_device(): full = lax.all_gather(two, 'head', axis=2, tiled=True)  69.9 us
    all_gather x2, waiting for transfers between devices, per_device(): full = lax.all_gather(one, 'head', axis=2, tiled=True)  42.4 us
    dot_general x6, matrix products, summed_columns(): jnp.dot(portion, row_block, preferred_element_type=jnp.float32).astype(BF16)  27.5 us
    all_to_all x2, blocking collectives, per_device(): lax.all_to_all(one, 'seq', split_axis=1, concat_axis=0, tiled=True)  26.3 us
    dot_general x9, matrix products, project_three(): jnp.dot(normed, weights[member], preferred_element_type=jnp.float32)  25.1 us
    pallas_call x2, Pallas kernels, temporal_attention(): pl.pallas_call(temporal_kernel, grid=(patches // group,), in_specs=[spec]...  21.6 us
  transfers between devices with their start and end apart: 11, of which 11 were waited for; matrix products, arithmetic and copies ran while one was open for 16% of the time, Pallas kernels for 5%

commit v1 on v0

v1 whole, which is shorter than its diff:
```python
import functools
import math

import jax
import jax.numpy as jnp
from jax import lax
from jax.experimental import pallas as pl
from jax.experimental.pallas import tpu as pltpu
from jax.sharding import PartitionSpec as P

HD = 64
PAIR = 128
CHUNKS = 4
AHEAD = 2
EXP2_SCALE = HD ** (-0.5) * math.log2(math.e)
GELU_SCALE = math.sqrt(2.0 / math.pi)
BF16 = jnp.bfloat16
F32 = jnp.float32
NT = (((1,), (1,)), ((), ()))
VMEM_LIMIT = 60 * 1024 * 1024
DMA = pltpu.SemaphoreType.DMA


def weighted_values(scores, values):
    top = jnp.max(scores, axis=-1, keepdims=True)
    weights = jnp.exp2((scores - top) * EXP2_SCALE).astype(BF16)
    extended = jnp.concatenate([values, jnp.ones_like(values)], axis=1)
    summed = jnp.dot(weights, extended, preferred_element_type=F32)
    return summed[:, :HD] / summed[:, HD:]


def gelu(x):
    return 0.5 * x * (1.0 + jnp.tanh(GELU_SCALE * (x + 0.044715 * (x * x * x))))


class Line:
    def __init__(self, n, gathered, partial, below, above, sems):
        self.n = n
        self.z = lax.axis_index("head")
        self.gathered, self.partial = gathered, partial
        self.below, self.above = below, above
        self.got, self.gave, self.from_below, self.from_above, self.passed = sems

    def barrier(self):
        sem = pltpu.get_barrier_semaphore()
        has_lower, has_upper = self.z > 0, self.z < self.n - 1

        @pl.when(has_lower)
        def _():
            pl.semaphore_signal(sem, inc=1, device_id={"head": self.z - 1})

        @pl.when(has_upper)
        def _():
            pl.semaphore_signal(sem, inc=1, device_id={"head": self.z + 1})

        pl.semaphore_wait(sem, has_lower.astype(jnp.int32) + has_upper.astype(jnp.int32))

    def piece(self, chunk, part, up):
        return pltpu.make_async_remote_copy(
            src_ref=self.gathered.at[chunk, part],
            dst_ref=self.gathered.at[chunk, part],
            send_sem=self.gave.at[0 if up else 1, chunk, part],
            recv_sem=self.got.at[chunk, part],
            device_id={"head": self.z + 1 if up else self.z - 1},
        )

    def give(self, chunk, part):
        @pl.when(self.z < self.n - 1)
        def _():
            self.piece(chunk, part, True).start()

        @pl.when(self.z > 0)
        def _():
            self.piece(chunk, part, False).start()

    def collect(self, chunk):
        z, n = self.z, self.n
        for step in range(1, n):

            @pl.when(z - step >= 0)
            def _():
                self.piece(chunk, z - step, True).wait_recv()

                @pl.when(z < n - 1)
                def _():
                    self.piece(chunk, z - step, True).start()

            @pl.when(z + step <= n - 1)
            def _():
                self.piece(chunk, z + step, False).wait_recv()

                @pl.when(z > 0)
                def _():
                    self.piece(chunk, z + step, False).start()

    def total(self, chunk, part, up):
        return pltpu.make_async_remote_copy(
            src_ref=self.partial.at[chunk, part],
            dst_ref=(self.below if up else self.above).at[chunk, part],
            send_sem=self.passed.at[chunk, part],
            recv_sem=(self.from_below if up else self.from_above).at[chunk, part],
            device_id={"head": self.z + 1 if up else self.z - 1},
        )

    def pass_on(self, chunk, lag):
        n = self.n

        def forward(part, up):
            if lag > 0:
                self.total(chunk, part, up).wait_recv()
                came = self.below if up else self.above
                self.partial[chunk, part] = (
                    self.partial[chunk, part].astype(F32) + came[chunk, part].astype(F32)
                ).astype(BF16)
            self.total(chunk, part, up).start()

        @pl.when(self.z == lag)
        def _():
            for part in range(n - 1, lag, -1):
                forward(part, True)

        @pl.when(self.z == n - 1 - lag)
        def _():
            for part in range(n - 1 - lag):
                forward(part, False)

    def finish(self, chunk, acc):
        z = self.z
        acc[...] = self.partial[chunk, z].astype(F32)

        @pl.when(z > 0)
        def _():
            self.total(chunk, z, True).wait_recv()
            acc[...] += self.below[chunk, z].astype(F32)

        @pl.when(z < self.n - 1)
        def _():
            self.total(chunk, z, False).wait_recv()
            acc[...] += self.above[chunk, z].astype(F32)

    def drain(self, chunk):
        z, n = self.z, self.n
        for part in range(n):

            @pl.when((z < n - 1) & (part <= z))
            def _():
                self.piece(chunk, part, True).wait_send()

            @pl.when((z > 0) & (part >= z))
            def _():
                self.piece(chunk, part, False).wait_send()

            @pl.when(part > z)
            def _():
                self.total(chunk, part, True).wait_send()

            @pl.when(part < z)
            def _():
                self.total(chunk, part, False).wait_send()


def normalise(gathered, chunk, mod, normed):
    n, rows, width = gathered.shape[1:]
    group = min(16, rows)

    def body(index, carry):
        here = pl.ds(pl.multiple_of(index * group, group), group)
        parts = [gathered[chunk, part, here, :].astype(F32) for part in range(n)]
        scale = 1.0 / (n * width)
        average = sum(jnp.sum(p, axis=-1, keepdims=True) for p in parts) * scale
        parts = [p - average for p in parts]
        variance = sum(jnp.sum(p * p, axis=-1, keepdims=True) for p in parts) * scale
        factor = lax.rsqrt(variance + 1e-06)
        for part in range(n):
            lanes = slice(part * width, (part + 1) * width)
            normed[here, lanes] = (
                parts[part] * factor * (1.0 + mod[1:2, lanes]) + mod[0:1, lanes]
            ).astype(BF16)
        return carry

    lax.fori_loop(0, rows // group, body, 0)


def project(source, weight, store, tile):
    columns = weight.shape[1]

    def body(index, carry):
        lanes = pl.ds(pl.multiple_of(index * tile, tile), tile)
        store(index, lanes, jnp.dot(source[...], weight[:, lanes], preferred_element_type=F32))
        return carry

    lax.fori_loop(0, columns // tile, body, 0)


def run_stage(line, chunks, x, out, mod, gate, acc, load_sem, weights, first, second):
    n, z = line.n, line.z
    gathered = line.gathered
    rows, width = gathered.shape[2:]
    frames = x.shape[0]
    piece = rows // frames

    def own(chunk, frame):
        return pltpu.make_async_copy(
            x.at[frame, pl.ds(pl.multiple_of(chunk * piece, piece), piece), :],
            gathered.at[chunk, z, pl.ds(frame * piece, piece), :],
            load_sem.at[chunk, frame],
        )

    for chunk in range(chunks):
        for frame in range(frames):
            own(chunk, frame).start()
    for copy in weights:
        copy.start()
    line.barrier()
    for chunk in range(chunks):
        for frame in range(frames):
            own(chunk, frame).wait()
        if chunk < AHEAD:
            line.give(chunk, z)

    def arrive(chunk):
        line.collect(chunk)

        @pl.when(chunk + AHEAD < chunks)
        def _():
            line.give(chunk + AHEAD, z)

    def pass_older(step):
        for lag in range(n - 1, 0, -1):
            chunk = step - lag

            @pl.when((chunk >= 0) & (chunk < chunks))
            def _():
                line.pass_on(chunk, lag)

    def complete(chunk):
        line.finish(chunk, acc)
        total = gathered[chunk, z].astype(F32) + gate[...] * acc[...]
        here = pl.ds(pl.multiple_of(chunk * piece, piece), piece)
        out[:, here, :] = total.astype(BF16).reshape(frames, piece, width)

    if first is not None:

        def gather_step(step, carry):
            arrive(step)

            @pl.when(step == 0)
            def _():
                for copy in weights:
                    copy.wait()

            first(step)
            return carry

        lax.fori_loop(0, chunks, gather_step, 0)

    def main_step(step, carry):
        if first is None:

            @pl.when(step < chunks)
            def _():
                arrive(step)

        pass_older(step)

        @pl.when(step < chunks)
        def _():
            if first is None:

                @pl.when(step == 0)
                def _():
                    for copy in weights:
                        copy.wait()

            second(step)
            line.pass_on(step, 0)

        @pl.when(step >= n - 1)
        def _():
            complete(step - (n - 1))

        return carry

    lax.fori_loop(0, chunks + n - 1, main_step, 0)

    def drain(chunk, carry):
        line.drain(chunk)
        return carry

    lax.fori_loop(0, chunks, drain, 0)


def spatial_kernel(n, chunks, x, w_in, w_out, mod, gate, out, gathered, partial, below, above, *rest):
    *sems, load_sem, w_sem, acc, normed, w_in_v, w_out_v, query, keys, values, mixed = rest
    line = Line(n, gathered, partial, below, above, sems)
    rows, width = gathered.shape[2:]
    weights = [
        pltpu.make_async_copy(w_in, w_in_v, w_sem.at[0]),
        pltpu.make_async_copy(w_out, w_out_v, w_sem.at[1]),
    ]

    def first(chunk):
        normalise(gathered, chunk, mod, normed)
        here = pl.ds(pl.multiple_of(chunk * rows, rows), rows)
        for member, target in enumerate((query, keys, values)):
            target[here, :] = jnp.dot(
                normed[...], w_in_v[member], preferred_element_type=F32
            ).astype(BF16)

    def second(chunk):
        here = pl.ds(pl.multiple_of(chunk * rows, rows), rows)

        def pair(index, carry):
            lanes = pl.ds(pl.multiple_of(index * PAIR, PAIR), PAIR)
            q, k, v = query[here, lanes], keys[:, lanes], values[:, lanes]
            outs = []
            for head in range(PAIR // HD):
                mine = slice(head * HD, (head + 1) * HD)
                scores = lax.dot_general(q[:, mine], k[:, mine], NT, preferred_element_type=F32)
                outs.append(weighted_values(scores, v[:, mine]))
            mixed[:, lanes] = jnp.concatenate(outs, axis=1).astype(BF16)
            return carry

        lax.fori_loop(0, width // PAIR, pair, 0)

        def store(index, lanes, value):
            partial[chunk, index] = value.astype(BF16)

        project(mixed, w_out_v, store, width)

    run_stage(line, chunks, x, out, mod, gate, acc, load_sem, weights, first, second)


def temporal_kernel(n, chunks, x, w_in, w_out, mod, gate, out, gathered, partial, below, above, *rest):
    *sems, load_sem, w_sem, acc, normed, w_in_v, w_out_v, query, keys, values, mixed = rest
    line = Line(n, gathered, partial, below, above, sems)
    rows, width = gathered.shape[2:]
    frames = x.shape[0]
    patches = rows // frames
    group = min(128 // frames, patches)
    weights = [
        pltpu.make_async_copy(w_in, w_in_v, w_sem.at[0]),
        pltpu.make_async_copy(w_out, w_out_v, w_sem.at[1]),
    ]

    def second(chunk):
        normalise(gathered, chunk, mod, normed)
        for member, target in enumerate((query, keys, values)):
            value = jnp.dot(normed[...], w_in_v[member], preferred_element_type=F32)
            target[...] = value.astype(BF16).reshape(frames, patches, width)
        size = frames * group
        row = lax.broadcasted_iota(jnp.int32, (size, size), 0)
        column = lax.broadcasted_iota(jnp.int32, (size, size), 1)
        same_patch = lax.rem(row, group) == lax.rem(column, group)
        for start in range(0, patches, group):
            here = slice(start, start + group)

            def pair(index, carry):
                lanes = pl.ds(pl.multiple_of(index * PAIR, PAIR), PAIR)
                q, k, v = [
                    source[:, here, lanes].reshape(size, PAIR) for source in (query, keys, values)
                ]
                outs = []
                for head in range(PAIR // HD):
                    mine = slice(head * HD, (head + 1) * HD)
                    scores = lax.dot_general(
                        q[:, mine], k[:, mine], NT, preferred_element_type=F32
                    )
                    outs.append(
                        weighted_values(jnp.where(same_patch, scores, -jnp.inf), v[:, mine])
                    )
                mixed[:, here, lanes] = (
                    jnp.concatenate(outs, axis=1).astype(BF16).reshape(frames, group, PAIR)
                )
                return carry

            lax.fori_loop(0, width // PAIR, pair, 0)
        source = mixed[...].reshape(rows, width)

        def body(index, carry):
            lanes = pl.ds(pl.multiple_of(index * width, width), width)
            partial[chunk, index] = jnp.dot(
                source, w_out_v[:, lanes], preferred_element_type=F32
            ).astype(BF16)
            return carry

        lax.fori_loop(0, n, body, 0)

    run_stage(line, chunks, x, out, mod, gate, acc, load_sem, weights, None, second)


def mlp_kernel(n, chunks, x, w_in, w_out, mod, gate, out, gathered, partial, below, above, *rest):
    *sems, load_sem, w_sem, acc, normed, w_in_v, w_out_v, hidden = rest
    line = Line(n, gathered, partial, below, above, sems)
    width = gathered.shape[3]
    weights = [
        pltpu.make_async_copy(w_in, w_in_v, w_sem.at[0]),
        pltpu.make_async_copy(w_out, w_out_v, w_sem.at[1]),
    ]

    def second(chunk):
        normalise(gathered, chunk, mod, normed)

        def keep(index, lanes, value):
            hidden[:, lanes] = gelu(value).astype(BF16)

        project(normed, w_in_v, keep, min(512, w_in_v.shape[1]))

        def store(index, lanes, value):
            partial[chunk, index] = value.astype(BF16)

        project(hidden, w_out_v, store, width)

    run_stage(line, chunks, x, out, mod, gate, acc, load_sem, weights, None, second)


def stage(kernel, name, number, x, w_in, w_out, mod, gate, extra, flops):
    n = lax.axis_size("head")
    frames, patches, width = x.shape
    chunks = CHUNKS
    rows = frames * patches // chunks
    model = n * width
    store = pltpu.VMEM((chunks, n, rows, width), BF16)
    any_space = pl.BlockSpec(memory_space=pl.ANY)
    vmem = pl.BlockSpec(memory_space=pltpu.VMEM)
    return pl.pallas_call(
        functools.partial(kernel, n, chunks),
        out_shape=jax.ShapeDtypeStruct(x.shape, BF16),
        in_specs=[any_space, any_space, any_space, vmem, vmem],
        out_specs=vmem,
        scratch_shapes=[
            store,
            store,
            store,
            store,
            DMA((chunks, n)),
            DMA((2, chunks, n)),
            DMA((chunks, n)),
            DMA((chunks, n)),
            DMA((chunks, n)),
            DMA((chunks, frames)),
            DMA((2,)),
            pltpu.VMEM((rows, width), F32),
            pltpu.VMEM((rows, model), BF16),
            pltpu.VMEM(w_in.shape, BF16),
            pltpu.VMEM(w_out.shape, BF16),
        ]
        + extra(rows),
        compiler_params=pltpu.CompilerParams(
            collective_id=number, has_side_effects=True, vmem_limit_bytes=VMEM_LIMIT
        ),
        cost_estimate=pl.CostEstimate(
            flops=flops, bytes_accessed=4 * x.size + 2 * (w_in.size + w_out.size), transcendentals=0
        ),
        name=name,
    )(x, w_in, w_out, mod, gate)


def per_device(
    latent,
    modulation,
    spatial_qkv,
    spatial_out,
    temporal_qkv,
    temporal_out,
    hidden_weight,
    output_weight,
):
    frames_local, patches, width = latent.shape
    seq = lax.axis_size("seq")
    part = patches // seq
    anchor = lax.axis_index("head") * width
    gates = lax.dynamic_slice_in_dim(modulation, anchor, width, 1)
    tokens = frames_local * patches

    def spatial_extra(rows):
        whole = pltpu.VMEM((tokens, width), BF16)
        return [whole, whole, whole, pltpu.VMEM((rows, width), BF16)]

    def temporal_extra(rows):
        frames = frames_local * seq
        return [pltpu.VMEM((frames, rows // frames, width), BF16)] * 4

    def mlp_extra(rows):
        return [pltpu.VMEM((rows, hidden_weight.shape[1]), BF16)]

    model = modulation.shape[1]
    base = 2 * tokens * model
    one = stage(
        spatial_kernel, "spatial", 0, latent.reshape(seq, part, width), spatial_qkv, spatial_out,
        modulation[0:2], gates[2:3], spatial_extra, base * 4 * width,
    )
    one = lax.all_to_all(one, "seq", split_axis=0, concat_axis=0, tiled=True)
    two = stage(
        temporal_kernel, "temporal", 1, one, temporal_qkv, temporal_out,
        modulation[3:5], gates[5:6], temporal_extra, base * 4 * width,
    )
    return stage(
        mlp_kernel, "mlp", 2, two, hidden_weight, output_weight,
        modulation[6:8], gates[8:9], mlp_extra, base * 2 * hidden_weight.shape[1],
    )


def solution(mesh):
    in_specs = (
        P("seq", None, "head"),
        P(),
        P(None, None, "head"),
        P("head", None),
        P(None, None, "head"),
        P("head", None),
        P(None, "head"),
        P("head", None),
    )
    out_specs = P(None, "seq", "head")
    return jax.shard_map(
        per_device, mesh=mesh, in_specs=in_specs, out_specs=out_specs, check_vma=False
    )
```

time: 594 us -> 435 us (0.73); the launches traced: 586 us -> 434 us
  waiting for transfers between devices: 379 us -> 0 us
  Pallas kernels: 42 us -> 409 us
  matrix products: 71.8 us -> 0 us
  other arithmetic: 40.8 us -> 0 us
  between operations: 14 us -> 0.03 us
  blocking collectives: 26.3 us -> 19.6 us
    pallas_call x4 -> x3, Pallas kernels: 42 us -> 409 us  [stage(): pl.pallas_call(functools.partial(kernel, n, chunks), out_shape=jax.ShapeD...]
    all_gather x5 -> x0, waiting for transfers between devices: 196 us -> none  [the longest x1 84 us: per_device(): full_spatial = lax.all_gather(latent, 'head', axis=2, tiled=True)]
    reduce_scatter x6 -> x0, waiting for transfers between devices: 181 us -> none  [summed_columns(): return lax.psum_scatter(partial, 'head', scatter_dimension=2, tiled=True)]
    dot_general x17 -> x0, matrix products: 71.8 us -> none  [the longest x6 27.5 us: summed_columns(): jnp.dot(portion, row_block, preferred_element_type=jnp.float32).astype(BF16)]
    reduce_sum x10 -> x0, other arithmetic: 22.6 us -> none  [the longest x5 11.3 us: layer_norm(): variance = jnp.mean(centred * centred, axis=-1, keepdims=True)]
    unnamed x7 -> x0, other arithmetic: 7.59 us -> none
    all_to_all x2 -> x1, blocking collectives: 26.3 us -> 19.6 us  [per_device(): one = lax.all_to_all(one, 'seq', split_axis=0, concat_axis=0, tiled=True)]
    convert_element_type x4 -> x0, other arithmetic: 6.44 us -> none  [add_branch(): (stream.astype(jnp.float32) + gate * reduced.astype(jnp.float32)).astype(...]
  transfers between devices with their start and end apart: 11 -> 0, of which waited for: 11 -> 0; matrix products, arithmetic and copies ran while one was open for 16% -> 0% of each run, Pallas kernels for 5% -> 0%
where the time goes in v1:
time: 435 us; the launch traced here: 434 us
  Pallas kernels  409 us (94%)
  blocking collectives  19.6 us (5%)
  local copies, waits for them, and re-layouts  5.28 us (1%)
    pallas_call x3, Pallas kernels, stage(): pl.pallas_call(functools.partial(kernel, n, chunks), out_shape=jax.ShapeD...  409 us
    all_to_all x1, blocking collectives, per_device(): one = lax.all_to_all(one, 'seq', split_axis=0, concat_axis=0, tiled=True)  19.6 us

profile of v1, /device:TPU:0, one launch (start us, length us, event | category | flops | bytes accessed | tf_op | source)
XLA Modules:
  0.0 433.9 jit_solution(4081285126975057147)
XLA Ops:
  0.0 1.6 fusion.1
  1.6 1.4 fusion
  3.0 159.6 %spatial.1 = bf16[8,128,512]{2,1,0:T(8,128)(2,1)} custom-call(bf16[8,128,512]{2,1,0:T(8,128)(2,1)} %bitcast.1, bf16[3,2048,512]{2,1,0:T(8,128)(2,1)} %w_in.3, bf16[512,2048]{1,0:T(8,128)(2,1)} %w_out.3, f32[2,2048]{1,0:T(2,128)} %get-tuple-element.9.mod, f32[1,512]{1,0:T(1,128)} %get-tuple-element.7.gate), custom_call_target="tpu_custom_call" | custom-call | flops 8589934592 | bytes 10485760 | tf_op jit(solution)/shard_map/spatial/pallas_call | solution.py:426
  162.6 19.6 %all_to_all.5.x = bf16[8,128,512]{2,1,0:T(8,128)(2,1)} all-to-all(bf16[8,128,512]{2,1,0:T(8,128)(2,1)} %spatial.1), channel_id=1, replica_groups=mesh['seq'=8,'head'=4] {'seq'}, dimensions={0} | all-to-all | bytes 2097152 | tf_op jit(solution)/shard_map/all_to_all | solution.py:493
  182.2 134.7 %temporal.1.x = bf16[8,128,512]{2,1,0:T(8,128)(2,1)} custom-call(bf16[8,128,512]{2,1,0:T(8,128)(2,1)} %all_to_all.5.x, bf16[3,2048,512]{2,1,0:T(8,128)(2,1)} %w_in.4, bf16[512,2048]{1,0:T(8,128)(2,1)} %w_out.4, f32[2,2048]{1,0:T(2,128)} %get-tuple-element.10.mod, f32[1,512]{1,0:T(1,128)} %get-tuple-element.6.gate), custom_call_target="tpu_custom_call" | custom-call | flops 8589934592 | bytes 10485760 | tf_op jit(solution)/shard_map/temporal/pallas_call | solution.py:426
  316.9 114.7 %mlp.1 = bf16[8,128,512]{2,1,0:T(8,128)(2,1)} custom-call(bf16[8,128,512]{2,1,0:T(8,128)(2,1)} %temporal.1.x, bf16[2048,2048]{1,0:T(8,128)(2,1)} %w_in.5, bf16[2048,2048]{1,0:T(8,128)(2,1)} %w_out.5, f32[2,2048]{1,0:T(2,128)} %get-tuple-element.8.mod, f32[1,512]{1,0:T(1,128)} %get-tuple-element.5.gate), custom_call_target="tpu_custom_call" | custom-call | flops 17179869184 | bytes 18874368 | tf_op jit(solution)/shard_map/mlp/pallas_call | solution.py:426
  431.7 2.3 copy.10
